TPU v7x, 32 devices: a whole 2x2x4 slice. The times are simulated.
32 devices in a mesh: group: 4 (over y, x), rank: 8 (over z, core).
Axes of the slice: x: 2, y: 2, z: 4, core: 2. Of those that a mesh axis runs over, the one named last changes fastest.
Arguments:
- queries: bfloat16 [8192, 2048], P(('group', 'rank')), may hold values from -32 to 32
- key_rows: bfloat16 [8192, 2048], P(('group', 'rank')), may hold values from -6 to 6
- value_rows: bfloat16 [8192, 2048], P(('group', 'rank')), may hold values from -6 to 6
- tile_links: int32 [64, 8], P(('group', 'rank')), may hold values from 0 to 15, as said below
- link_counts: int32 [64], P(('group', 'rank')), may hold values from 1 to 8, 256 in all
Outputs:
- attended: bfloat16 [8192, 2048], P(('group', 'rank'))
Inputs may be any that keep to these rules, and one draw needn't show every extreme that they name: `tile_links`: each row names 8 different candidates.
All inputs are finite; a program needn't handle non-finite values. No bound on the sum of `link_counts` on one device may be relied on, other than what follows from the above.
Results may differ from a plain program's by a relative error of at most 0.0045.
Values may be sent and summed in bfloat16 or wider, within the bound.
A program may use at most 128 MiB of HBM per device.

v0:
```python
import functools
import math

import jax
import jax.numpy as jnp
from jax import lax
from jax.experimental import pallas as pl
from jax.experimental.pallas import tpu as pltpu
from jax.sharding import PartitionSpec as P

HD = 128
CHUNK_SIXTEENTHS = (4, 4, 4, 2, 1, 1)
MESH = pl.DeviceIdType.MESH


def kernel(
    groups,
    ranks,
    bounds,
    q_hbm,
    k_hbm,
    v_hbm,
    links_hbm,
    counts_hbm,
    o_ref,
    land,
    q_v,
    bias,
    send_sems,
    recv_sems,
    q_sem,
    links,
    counts,
    list_sems,
):
    _, slots, rows, _ = land.shape
    chunks = len(bounds) - 1
    tiles, lmax = links.shape
    tile_rows = rows // tiles
    g = lax.axis_index("group")
    r = lax.axis_index("rank")
    core = lax.rem(r, 2)
    partner = (g, r + 1 - 2 * core)
    upper = (2 * r) // ranks
    first = (g, lax.rem(r + ranks - 2 + 4 * upper, ranks))
    second = (g, lax.rem(r + ranks + 2 - 4 * upper, ranks))
    flows = [(first, 4 - 3 * upper), (second, 1 + 3 * upper)]
    crossed = groups == 4
    across = (g + 1 - 2 * lax.rem(g, 2), lax.rem(g + 2, 4))

    def peer_slot(source, at):
        return 4 + lax.rem(source - at + groups, groups)

    if crossed:
        for near in across:
            flows.append(((near, r), peer_slot(g, near)))
    else:
        for step in range(1, groups):
            flows.append(((lax.rem(g + groups - step, groups), r), 4 + step))
    flows.append((partner, 2 + core))
    relay = len(flows)
    hops = (across, across[::-1])

    barrier = pltpu.get_barrier_semaphore()
    for device, _ in flows:
        pl.semaphore_signal(barrier, inc=1, device_id=device, device_id_type=MESH)

    def columns(c):
        return pl.ds(bounds[c] * HD, (bounds[c + 1] - bounds[c]) * HD)

    def own_copy(c, kv):
        src = (k_hbm, v_hbm)[kv]
        return pltpu.make_async_copy(
            src.at[:, columns(c)], land.at[kv, 0, :, columns(c)], recv_sems.at[c, kv, 0]
        )

    def flow_copy(c, kv, f):
        device, slot = flows[f]
        src = (k_hbm, v_hbm)[kv]
        return pltpu.make_async_remote_copy(
            src_ref=src.at[:, columns(c)],
            dst_ref=land.at[kv, slot, :, columns(c)],
            send_sem=send_sems.at[c, kv, f],
            recv_sem=recv_sems.at[c, kv, slot],
            device_id=device,
            device_id_type=MESH,
        )

    def relay_copy(c, kv):
        return pltpu.make_async_remote_copy(
            src_ref=land.at[kv, 4 - 3 * core, :, columns(c)],
            dst_ref=land.at[kv, 3 - core, :, columns(c)],
            send_sem=send_sems.at[c, kv, relay],
            recv_sem=recv_sems.at[c, kv, 3 - core],
            device_id=partner,
            device_id_type=MESH,
        )

    def cross_copy(c, kv):
        source, target = hops[kv]
        slot = peer_slot(source, target)
        return pltpu.make_async_remote_copy(
            src_ref=land.at[kv, peer_slot(source, g), :, columns(c)],
            dst_ref=land.at[kv, slot, :, columns(c)],
            send_sem=send_sems.at[c, kv, relay + 1],
            recv_sem=recv_sems.at[c, kv, slot],
            device_id=(target, r),
            device_id_type=MESH,
        )

    def arrived(c, kv, slot):
        pltpu.make_async_remote_copy(
            src_ref=land.at[kv, slot, :, columns(c)],
            dst_ref=land.at[kv, slot, :, columns(c)],
            send_sem=send_sems.at[c, kv, 0],
            recv_sem=recv_sems.at[c, kv, slot],
            device_id=partner,
            device_id_type=MESH,
        ).wait_recv()

    def issue(c):
        for kv in range(2):
            for f in range(len(flows)):
                flow_copy(c, kv, f).start()

    local = [
        pltpu.make_async_copy(q_hbm, q_v, q_sem),
        pltpu.make_async_copy(links_hbm, links, list_sems.at[0]),
        pltpu.make_async_copy(counts_hbm, counts, list_sems.at[1]),
    ]
    for copy in local:
        copy.start()
    pl.semaphore_wait(barrier, len(flows))

    for c in range(chunks):
        issue(c)
    for c in range(chunks):
        for kv in range(2):
            own_copy(c, kv).start()

    for copy in local:
        copy.wait()
    cand = lax.broadcasted_iota(jnp.int32, (1, slots * rows), 1) // tile_rows
    for i in range(tiles):
        used = jnp.where(cand == i, 1, 0)
        for j in range(lmax):
            hit = jnp.where(j < counts[i], links[i, j], -1)
            used = used + jnp.where(cand == hit, 1, 0)
        bias[i, :, :] = jnp.where(used == 0, -jnp.inf, jnp.where(used == 2, 1.0, 0.0))

    scale = HD ** (-0.5) * math.log2(math.e)

    def attend(c):
        @pl.loop(bounds[c], bounds[c + 1])
        def _(h):
            head = pl.ds(pl.multiple_of(h * HD, HD), HD)
            keys = land[0, :, :, head].reshape(slots * rows, HD)
            values = land[1, :, :, head].reshape(slots * rows, HD)
            scores = lax.dot_general(
                q_v[:, head], keys, (((1,), (1,)), ((), ())), preferred_element_type=jnp.float32
            )
            scores = scores.reshape(tiles, tile_rows, slots * rows) * scale + bias[...]
            scores = scores.reshape(rows, slots * rows)
            weights = jnp.exp2(scores - jnp.max(scores, axis=1, keepdims=True))
            total = jnp.sum(weights, axis=1, keepdims=True)
            mixed = jnp.dot(
                weights.astype(jnp.bfloat16), values, preferred_element_type=jnp.float32
            )
            o_ref[:, head] = (mixed / total).astype(jnp.bfloat16)

    for c in range(chunks + 1):
        if c < chunks:
            for kv in range(2):
                arrived(c, kv, 4 - 3 * core)
                relay_copy(c, kv).start()
                if crossed:
                    arrived(c, kv, peer_slot(hops[kv][0], g))
                    cross_copy(c, kv).start()
        if c >= 1:
            b = c - 1
            for kv in range(2):
                own_copy(b, kv).wait()
                arrived(b, kv, 1 + 3 * core)
                for slot in (2, 3):
                    arrived(b, kv, slot)
                if crossed:
                    arrived(b, kv, peer_slot(hops[kv][1], g))
                    arrived(b, kv, peer_slot(3 - g, g))
                else:
                    for slot in range(5, slots):
                        arrived(b, kv, slot)
            attend(b)

    for c in range(chunks):
        for kv in range(2):
            for f in range(len(flows)):
                flow_copy(c, kv, f).wait_send()
            relay_copy(c, kv).wait_send()
            if crossed:
                cross_copy(c, kv).wait_send()


def shards(groups, ranks, queries, key_rows, value_rows, tile_links, link_counts):
    rows, features = queries.shape
    tiles = tile_links.shape[0]
    slots = 4 + groups
    heads = features // HD
    bounds = [0]
    for part in CHUNK_SIXTEENTHS:
        bounds.append(bounds[-1] + part * heads // 16)
    chunks = len(bounds) - 1
    hbm = pl.BlockSpec(memory_space=pl.ANY)
    return pl.pallas_call(
        functools.partial(kernel, groups, ranks, tuple(bounds)),
        out_shape=jax.ShapeDtypeStruct((rows, features), jnp.bfloat16),
        in_specs=[hbm] * 5,
        out_specs=pl.BlockSpec(memory_space=pltpu.VMEM),
        scratch_shapes=[
            pltpu.VMEM((2, slots, rows, features), jnp.bfloat16),
            pltpu.VMEM((rows, features), jnp.bfloat16),
            pltpu.VMEM((tiles, 1, slots * rows), jnp.float32),
            pltpu.SemaphoreType.DMA((chunks, 2, groups + 4)),
            pltpu.SemaphoreType.DMA((chunks, 2, slots + 1)),
            pltpu.SemaphoreType.DMA,
            pltpu.SMEM(tile_links.shape, jnp.int32),
            pltpu.SMEM(link_counts.shape, jnp.int32),
            pltpu.SemaphoreType.DMA((2,)),
        ],
        compiler_params=pltpu.CompilerParams(
            collective_id=0, has_side_effects=True, vmem_limit_bytes=62 * 2**20
        ),
    )(queries, key_rows, value_rows, tile_links, link_counts)


def solution(mesh):
    nodes = P(("group", "rank"), None)
    return jax.shard_map(
        functools.partial(shards, mesh.shape["group"], mesh.shape["rank"]),
        mesh=mesh,
        in_specs=(nodes, nodes, nodes, nodes, P(("group", "rank"))),
        out_specs=nodes,
        check_vma=False,
    )
```

profile of v0, /device:TPU:1, one launch (start us, length us, event | category | flops | bytes accessed | tf_op | source)
XLA Modules:
  0.0 103.5 jit_solution(16439287738624565986)
XLA Ops:
  0.0 101.2 %shard_map.55 = bf16[256,2048]{1,0:T(8,128)(2,1)} custom-call(bf16[256,2048]{1,0:T(8,128)(2,1)} %q_hbm.1, bf16[256,2048]{1,0:T(8,128)(2,1)} %k_hbm.1, bf16[256,2048]{1,0:T(8,128)(2,1)} %v_hbm.1, s32[2,8]{1,0:T(2,128)} %links_hbm.1, s32[2]{0:T(128)} %counts_hbm.1), custom_call_target="tpu_custom_call" | custom-call | tf_op jit(solution)/shard_map/pallas_call | solution.py:213
  101.2 2.3 %copy.7 = bf16[256,2048]{1,0:T(8,128)(2,1)} copy(bf16[256,2048]{1,0:T(8,128)(2,1)} %shard_map.55) | data formatting | bytes 2097152
where the time goes:
time: 104 us; the launch traced here: 103 us
  Pallas kernels  101 us (97%)
  local copies, waits for them, and re-layouts  2.3 us (2%)
    pallas_call x1, Pallas kernels, shards(): pl.pallas_call(functools.partial(kernel, groups, ranks, tuple(bounds)), o...  101 us
    unnamed x1, local copies, waits for them, and re-layouts  2.3 us

commit v1 on v0

v1 whole, which is shorter than its diff:
```python
import functools
import math

import jax
import jax.numpy as jnp
from jax import lax
from jax.experimental import pallas as pl
from jax.experimental.pallas import tpu as pltpu
from jax.sharding import PartitionSpec as P

HD = 128
CHUNK_SIXTEENTHS = (4, 4, 4, 2, 1, 1)
MESH = pl.DeviceIdType.MESH


def kernel(
    groups,
    ranks,
    bounds,
    q_hbm,
    k_hbm,
    v_hbm,
    links_hbm,
    counts_hbm,
    o_ref,
    land,
    q_v,
    bias,
    send_sems,
    recv_sems,
    q_sem,
    links,
    counts,
    list_sems,
    ready,
):
    _, slots, rows, _ = land.shape
    chunks = len(bounds) - 1
    tiles, lmax = links.shape
    tile_rows = rows // tiles
    g = lax.axis_index("group")
    r = lax.axis_index("rank")
    core = lax.rem(r, 2)
    partner = (g, r + 1 - 2 * core)
    crossed = groups == 4
    across = (g + 1 - 2 * lax.rem(g, 2), lax.rem(g + 2, 4))

    def peer_slot(source, at):
        return 4 + lax.rem(source - at + groups, groups)

    flows = [
        ((g, lax.rem(r + 2, ranks)), 1, 1),
        ((g, lax.rem(r + ranks - 2, ranks)), 4, 0),
    ]
    if crossed:
        for near in across:
            flows.append(((near, r), peer_slot(g, near), len(flows)))
    else:
        for step in range(1, groups):
            back = 1 + groups - step
            flows.append(((lax.rem(g + groups - step, groups), r), 4 + step, back))
    beside = len(flows)
    relay = beside + 1
    hops = (across, across[::-1])

    here = g * ranks + r
    before = [target[0] * ranks + target[1] < here for target, _, _ in flows]
    barrier = pltpu.get_barrier_semaphore()
    pl.semaphore_signal(barrier, inc=1, device_id=partner, device_id_type=MESH)
    greeted = 1
    for (device, _, _), earlier in zip(flows, before):
        greeted = greeted + jnp.where(earlier, 1, 0)

        @pl.when(jnp.logical_not(earlier))
        def _():
            pl.semaphore_signal(barrier, inc=1, device_id=device, device_id_type=MESH)

    def columns(c):
        return pl.ds(bounds[c] * HD, (bounds[c + 1] - bounds[c]) * HD)

    def own_copy(c, kv):
        src = (k_hbm, v_hbm)[kv]
        return pltpu.make_async_copy(
            src.at[:, columns(c)], land.at[kv, 0, :, columns(c)], recv_sems.at[c, kv, 0]
        )

    def flow_copy(c, kv, f):
        device, slot = (partner, 2 + core) if f == beside else flows[f][:2]
        src = (k_hbm, v_hbm)[kv]
        part = columns(c)
        return pltpu.make_async_remote_copy(
            src_ref=src.at[:, part],
            dst_ref=land.at[kv, slot, :, part],
            send_sem=send_sems.at[kv, f],
            recv_sem=recv_sems.at[c, kv, slot],
            device_id=device,
            device_id_type=MESH,
        )

    def relay_copy(c, kv):
        return pltpu.make_async_remote_copy(
            src_ref=land.at[kv, 4 - 3 * core, :, columns(c)],
            dst_ref=land.at[kv, 3 - core, :, columns(c)],
            send_sem=send_sems.at[kv, relay],
            recv_sem=recv_sems.at[c, kv, 3 - core],
            device_id=partner,
            device_id_type=MESH,
        )

    def cross_copy(c, kv):
        source, target = hops[kv]
        slot = peer_slot(source, target)
        return pltpu.make_async_remote_copy(
            src_ref=land.at[kv, peer_slot(source, g), :, columns(c)],
            dst_ref=land.at[kv, slot, :, columns(c)],
            send_sem=send_sems.at[kv, relay + 1],
            recv_sem=recv_sems.at[c, kv, slot],
            device_id=(target, r),
            device_id_type=MESH,
        )

    def arrived(c, kv, slot):
        pltpu.make_async_remote_copy(
            src_ref=land.at[kv, slot, :, columns(c)],
            dst_ref=land.at[kv, slot, :, columns(c)],
            send_sem=send_sems.at[kv, 0],
            recv_sem=recv_sems.at[c, kv, slot],
            device_id=partner,
            device_id_type=MESH,
        ).wait_recv()

    def sent(kv, f):
        whole = land.at[kv, 0]
        pltpu.make_async_remote_copy(
            src_ref=whole,
            dst_ref=whole,
            send_sem=send_sems.at[kv, f],
            recv_sem=recv_sems.at[0, kv, 0],
            device_id=partner,
            device_id_type=MESH,
        ).wait_send()

    def issue(c, f):
        for kv in range(2):
            flow_copy(c, kv, f).start()

    local = [
        pltpu.make_async_copy(q_hbm, q_v, q_sem),
        pltpu.make_async_copy(links_hbm, links, list_sems.at[0]),
        pltpu.make_async_copy(counts_hbm, counts, list_sems.at[1]),
    ]
    for copy in local:
        copy.start()
    pl.semaphore_wait(barrier, greeted)

    for f, (device, _, back) in enumerate(flows):

        @pl.when(before[f])
        def _():
            pl.semaphore_signal(
                ready.at[back], inc=1, device_id=device, device_id_type=MESH
            )
            issue(0, f)

    issue(0, beside)
    for f in (0, *range(2, beside), 1):

        @pl.when(jnp.logical_not(before[f]))
        def _():
            pl.semaphore_wait(ready.at[f], 1)
            issue(0, f)

    for c in range(1, chunks):
        for f in range(beside + 1):
            issue(c, f)
    for c in range(chunks):
        for kv in range(2):
            own_copy(c, kv).start()

    for copy in local:
        copy.wait()
    cand = lax.broadcasted_iota(jnp.int32, (1, slots * rows), 1) // tile_rows
    for i in range(tiles):
        used = jnp.where(cand == i, 1, 0)
        for j in range(lmax):
            hit = jnp.where(j < counts[i], links[i, j], -1)
            used = used + jnp.where(cand == hit, 1, 0)
        bias[i, :, :] = jnp.where(used == 0, -jnp.inf, jnp.where(used == 2, 1.0, 0.0))

    scale = HD ** (-0.5) * math.log2(math.e)

    def weigh(head):
        keys = land[0, :, :, head].reshape(slots * rows, HD)
        scores = lax.dot_general(
            q_v[:, head], keys, (((1,), (1,)), ((), ())), preferred_element_type=jnp.float32
        )
        scores = scores.reshape(tiles, tile_rows, slots * rows) * scale + bias[...]
        scores = scores.reshape(rows, slots * rows)
        weights = jnp.exp2(scores - jnp.max(scores, axis=1, keepdims=True))
        return weights.astype(jnp.bfloat16), jnp.sum(weights, axis=1, keepdims=True)

    def mix(head, weights, total):
        values = land[1, :, :, head].reshape(slots * rows, HD)
        mixed = jnp.dot(weights, values, preferred_element_type=jnp.float32)
        o_ref[:, head] = (mixed / total).astype(jnp.bfloat16)

    def attend(c):
        @pl.loop(bounds[c], bounds[c + 1])
        def _(h):
            head = pl.ds(pl.multiple_of(h * HD, HD), HD)
            mix(head, *weigh(head))

    def pass_beside(c, kv):
        arrived(c, kv, 4 - 3 * core)
        relay_copy(c, kv).start()

    def pass_across(c, kv):
        if crossed:
            arrived(c, kv, peer_slot(hops[kv][0], g))
            cross_copy(c, kv).start()

    def gather(c, kv):
        own_copy(c, kv).wait()
        if crossed:
            arrived(c, kv, peer_slot(hops[kv][1], g))
            arrived(c, kv, peer_slot(3 - g, g))
        else:
            for slot in range(5, slots):
                arrived(c, kv, slot)
        arrived(c, kv, 1 + 3 * core)
        for slot in (2, 3):
            arrived(c, kv, slot)

    last = chunks - 1
    for kv in range(2):
        pass_across(0, kv)
    for c in range(last):
        for kv in range(2):
            pass_beside(c, kv)
        for kv in range(2):
            pass_across(c + 1, kv)
        if c >= 1:
            for kv in range(2):
                gather(c - 1, kv)
            attend(c - 1)
    for kv in range(2):
        gather(last - 1, kv)
    attend(last - 1)

    heads = [pl.ds(h * HD, HD) for h in range(bounds[last], bounds[chunks])]
    pass_beside(last, 0)
    gather(last, 0)
    parts = [weigh(head) for head in heads]
    pass_beside(last, 1)
    gather(last, 1)
    for head, part in zip(heads, parts):
        mix(head, *part)

    for kv in range(2):
        for f in range(relay + 1 + crossed):
            sent(kv, f)


def shards(groups, ranks, *operands):
    queries, _, _, tile_links, link_counts = operands
    rows, features = queries.shape
    tiles = tile_links.shape[0]
    slots = 4 + groups
    heads = features // HD
    bounds = [0]
    for part in CHUNK_SIXTEENTHS:
        bounds.append(bounds[-1] + part * heads // 16)
    chunks = len(bounds) - 1
    hbm = pl.BlockSpec(memory_space=pl.ANY)
    return pl.pallas_call(
        functools.partial(kernel, groups, ranks, tuple(bounds)),
        out_shape=jax.ShapeDtypeStruct((rows, features), jnp.bfloat16),
        in_specs=[hbm] * 5,
        out_specs=pl.BlockSpec(memory_space=pltpu.VMEM),
        scratch_shapes=[
            pltpu.VMEM((2, slots, rows, features), jnp.bfloat16),
            pltpu.VMEM((rows, features), jnp.bfloat16),
            pltpu.VMEM((tiles, 1, slots * rows), jnp.float32),
            pltpu.SemaphoreType.DMA((2, groups + 4)),
            pltpu.SemaphoreType.DMA((chunks, 2, slots + 1)),
            pltpu.SemaphoreType.DMA,
            pltpu.SMEM(tile_links.shape, jnp.int32),
            pltpu.SMEM(link_counts.shape, jnp.int32),
            pltpu.SemaphoreType.DMA((2,)),
            pltpu.SemaphoreType.REGULAR((groups + 1,)),
        ],
        compiler_params=pltpu.CompilerParams(
            collective_id=0, has_side_effects=True, vmem_limit_bytes=28 * 2**20
        ),
    )(*(pltpu.with_memory_space_constraint(a, pltpu.HBM) for a in operands))


def solution(mesh):
    nodes = P(("group", "rank"), None)
    return jax.shard_map(
        functools.partial(shards, mesh.shape["group"], mesh.shape["rank"]),
        mesh=mesh,
        in_specs=(nodes, nodes, nodes, nodes, P(("group", "rank"))),
        out_specs=nodes,
        check_vma=False,
    )
```

time: 104 us -> 98.3 us (0.945)
  Pallas kernels: 101 us -> 96.8 us
  local copies, waits for them, and re-layouts: 2.3 us -> 0.97 us
    pallas_call x1, Pallas kernels: 101 us -> 96.8 us  [shards(): pl.pallas_call(functools.partial(kernel, groups, ranks, tuple(bounds)), o...]
    unnamed x1, local copies, waits for them, and re-layouts: 2.3 us -> 0.97 us
where the time goes in v1:
time: 98.3 us; the launch traced here: 97.8 us
  Pallas kernels  96.8 us (98%)
    pallas_call x1, Pallas kernels, shards(): pl.pallas_call(functools.partial(kernel, groups, ranks, tuple(bounds)), o...  96.8 us

profile of v1, /device:TPU:1, one launch (start us, length us, event | category | flops | bytes accessed | tf_op | source)
XLA Modules:
  0.0 97.8 jit_solution(9005386115172306738)
XLA Ops:
  0.0 96.8 %shard_map.55 = bf16[256,2048]{1,0:T(8,128)(2,1)S(1)} custom-call(bf16[256,2048]{1,0:T(8,128)(2,1)} %q_hbm.1, bf16[256,2048]{1,0:T(8,128)(2,1)} %k_hbm.1, bf16[256,2048]{1,0:T(8,128)(2,1)} %v_hbm.1, s32[2,8]{1,0:T(2,128)} %links_hbm.1, s32[2]{0:T(128)} %counts_hbm.1), custom_call_target="tpu_custom_call" | custom-call | tf_op jit(solution)/shard_map/pallas_call | solution.py:275
  96.8 1.0 copy.7

commit v2 on v1

v2 whole, which is shorter than its diff:
```python
import functools
import math

import jax
import jax.numpy as jnp
from jax import lax
from jax.experimental import pallas as pl
from jax.experimental.pallas import tpu as pltpu
from jax.sharding import PartitionSpec as P

HD = 128
CHUNK_SIXTEENTHS = (9, 5, 1, 1)
MESH = pl.DeviceIdType.MESH
NEAR, ACROSS_K, ACROSS_V, REST, NEAR_V, REST_V, LATE = range(7)


def kernel(
    groups,
    ranks,
    bounds,
    q_hbm,
    k_hbm,
    v_hbm,
    links_hbm,
    counts_hbm,
    o_ref,
    land,
    q_v,
    bias,
    send_sem,
    recv_sems,
    ready,
    links,
    counts,
    local_sems,
):
    _, slots, rows, _ = land.shape
    chunks = len(bounds) - 1
    last = chunks - 1
    beat = min(1, last)
    tiles, lmax = links.shape
    tile_rows = rows // tiles
    g = lax.axis_index("group")
    r = lax.axis_index("rank")
    core = lax.rem(r, 2)
    partner = (g, r + 1 - 2 * core)
    crossed = groups == 4
    across = (g + 1 - 2 * lax.rem(g, 2), lax.rem(g + 2, 4))
    source = (k_hbm, v_hbm)

    def peer_slot(source, at):
        return 4 + lax.rem(source - at + groups, groups)

    flows = [
        ((g, lax.rem(r + 2, ranks)), 1, 1),
        ((g, lax.rem(r + ranks - 2, ranks)), 4, 0),
    ]
    if crossed:
        for other in across:
            flows.append(((other, r), peer_slot(g, other), len(flows)))
    else:
        for step in range(1, groups):
            back = 1 + groups - step
            flows.append(((lax.rem(g + groups - step, groups), r), 4 + step, back))
    hops = (across, across[::-1])
    near = 4 - 3 * core

    here = g * ranks + r
    before = [target[0] * ranks + target[1] < here for target, _, _ in flows]
    upper = 2 * r >= ranks
    inner = jnp.logical_and(r >= 2, r + 2 < ranks)
    second = [
        jnp.logical_and(inner, core == 0),
        jnp.logical_and(inner, core == 1),
        *(jnp.bool_(False) for _ in flows[2:]),
    ]
    barrier = pltpu.get_barrier_semaphore()
    pl.semaphore_signal(barrier, inc=1, device_id=partner, device_id_type=MESH)
    greeted = 1
    for (device, _, _), earlier in zip(flows, before):
        greeted = greeted + jnp.where(earlier, 1, 0)

        @pl.when(jnp.logical_not(earlier))
        def _():
            pl.semaphore_signal(barrier, inc=1, device_id=device, device_id_type=MESH)

    def columns(c):
        return pl.ds(bounds[c] * HD, (bounds[c + 1] - bounds[c]) * HD)

    def remote(src, dst, sem, device):
        return pltpu.make_async_remote_copy(
            src_ref=src,
            dst_ref=dst,
            send_sem=send_sem,
            recv_sem=sem,
            device_id=device,
            device_id_type=MESH,
        )

    def take(c, kind, ref):
        remote(ref, ref, recv_sems.at[c, kind], partner).wait_recv()

    def rest_of(c, kv):
        return REST_V if c == last and kv == 1 else REST

    def near_of(c, kv):
        return NEAR_V if c == last and kv == 1 else NEAR

    def flow(c, f):
        device, slot, _ = flows[f]
        for kv in range(2):
            if f < 2:
                other = LATE if c == last and kv == 1 else REST
                kind = jnp.where(core == 1 - f, near_of(c, kv), other)
            elif crossed and f - 2 == kv:
                kind = (ACROSS_K, ACROSS_V)[kv]
            else:
                kind = rest_of(c, kv)
            src = source[kv].at[:, columns(c)]
            dst = land.at[kv, slot, :, columns(c)]
            remote(src, dst, recv_sems.at[c, kind], device).start()

    def flow_beside(c):
        for kv in range(2):
            kind = NEAR_V if c == beat and c < last else rest_of(c, kv)
            src = source[kv].at[:, columns(c)]
            dst = land.at[kv, 2 + core, :, columns(c)]
            remote(src, dst, recv_sems.at[c, kind], partner).start()

    def pass_beside(c, kv=slice(None)):
        own = land.at[kv, near, :, columns(c)]
        take(c, NEAR if kv == slice(None) else near_of(c, kv), own)
        kind = REST if kv != 1 else LATE
        dst = land.at[kv, 3 - core, :, columns(c)]
        remote(own, dst, recv_sems.at[c, kind], partner).start()

    def pass_across(c):
        for kv in range(2 if crossed else 0):
            origin, target = hops[kv]
            own = land.at[kv, peer_slot(origin, g), :, columns(c)]
            take(c, (ACROSS_K, ACROSS_V)[kv], own)
            dst = land.at[kv, peer_slot(origin, target), :, columns(c)]
            remote(own, dst, recv_sems.at[c, rest_of(c, kv)], (target, r)).start()

    others = slots - 3 if crossed else slots - 2

    def gather(c):
        expected = others - 1 if c == beat and c < last else others
        take(c, REST, land.at[:, 0:expected, :, columns(c)])

    local = [
        pltpu.make_async_copy(src, dst, local_sems.at[i])
        for i, (src, dst) in enumerate(
            (
                (q_hbm, q_v),
                (links_hbm, links),
                (counts_hbm, counts),
                (k_hbm, land.at[0, 0]),
                (v_hbm, land.at[1, 0]),
            )
        )
    ]
    for copy in local[:3]:
        copy.start()
    pl.semaphore_wait(barrier, greeted)

    flow_beside(beat)
    for f, (device, _, back) in enumerate(flows):

        @pl.when(before[f])
        def _():
            pl.semaphore_signal(
                ready.at[back], inc=1, device_id=device, device_id_type=MESH
            )

        @pl.when(jnp.logical_and(before[f], jnp.logical_not(second[f])))
        def _():
            flow(0, f)

    for f in (0, *range(2, len(flows))):

        @pl.when(jnp.logical_not(before[f]))
        def _():
            pl.semaphore_wait(ready.at[f], 1)

        @pl.when(jnp.logical_not(jnp.logical_or(before[f], second[f])))
        def _():
            flow(0, f)

    if beat < last:
        take(beat, NEAR_V, land.at[:, 3 - core, :, columns(beat)])

    @pl.when(second[0])
    def _():
        flow(0, 0)

    @pl.when(jnp.logical_not(before[1]))
    def _():
        pl.semaphore_wait(ready.at[1], 1)

    @pl.when(jnp.logical_or(second[1], jnp.logical_not(before[1])))
    def _():
        flow(0, 1)

    for c in range(1, chunks):
        if c < last:
            flow(c, 0)
            flow(c, 1)
        else:

            @pl.when(upper)
            def _():
                flow(c, 0)
                flow(c, 1)

            @pl.when(jnp.logical_not(upper))
            def _():
                flow(c, 1)
                flow(c, 0)

        for f in range(2, len(flows)):
            flow(c, f)
    for c in range(chunks):
        if c != beat:
            flow_beside(c)
    for copy in local[3:]:
        copy.start()
    for copy in local:
        copy.wait()

    cand = lax.broadcasted_iota(jnp.int32, (1, slots * rows), 1) // tile_rows
    for i in range(tiles):
        used = jnp.where(cand == i, 1, 0)
        for j in range(lmax):
            hit = jnp.where(j < counts[i], links[i, j], -1)
            used = used + jnp.where(cand == hit, 1, 0)
        bias[i, :, :] = jnp.where(used == 0, -jnp.inf, jnp.where(used == 2, 1.0, 0.0))

    scale = HD ** (-0.5) * math.log2(math.e)

    def weigh(head):
        keys = land[0, :, :, head].reshape(slots * rows, HD)
        scores = lax.dot_general(
            q_v[:, head], keys, (((1,), (1,)), ((), ())), preferred_element_type=jnp.float32
        )
        scores = scores.reshape(tiles, tile_rows, slots * rows) * scale + bias[...]
        scores = scores.reshape(rows, slots * rows)
        weights = jnp.exp2(scores - jnp.max(scores, axis=1, keepdims=True))
        return weights.astype(jnp.bfloat16), jnp.sum(weights, axis=1, keepdims=True)

    def mix(head, weights, first, end):
        values = land[1, first:end, :, head].reshape((end - first) * rows, HD)
        part = weights[:, first * rows : end * rows]
        return jnp.dot(part, values, preferred_element_type=jnp.float32)

    def attend(heads):
        heads = [pl.ds(pl.multiple_of(h * HD, HD), HD) for h in heads]
        for head, (weights, total) in zip(heads, [weigh(head) for head in heads]):
            mixed = mix(head, weights, 0, slots)
            o_ref[:, head] = (mixed / total).astype(jnp.bfloat16)

    def attend_all(first, end):
        pairs = (end - first) // 2

        @pl.loop(0, pairs)
        def _(i):
            attend([first + 2 * i, first + 2 * i + 1])

        if first + 2 * pairs < end:
            attend([end - 1])

    pass_across(0)
    for c in range(last):
        pass_beside(c)
        pass_across(c + 1)
        gather(c)
        if c < last - 1:
            attend_all(bounds[c], bounds[c + 1])

    heads = [pl.ds(h * HD, HD) for h in range(bounds[last], bounds[chunks])]
    part = columns(last)
    middle = (bounds[last - 1] + bounds[last] + 1) // 2
    attend_all(bounds[last - 1], middle)
    pass_beside(last, 0)
    attend_all(middle, bounds[last])
    pass_beside(last, 1)
    take(last, REST, land.at[0, 0:others, :, part])
    weighed = [weigh(head) for head in heads]
    take(last, REST_V, land.at[1, 0 : others - 2, :, part])
    mixed = [
        mix(head, weights, 0, 1) + mix(head, weights, 5, slots)
        for head, (weights, _) in zip(heads, weighed)
    ]
    take(last, LATE, land.at[1, 0:2, :, part])
    for head, (weights, total), early in zip(heads, weighed, mixed):
        o_ref[:, head] = ((early + mix(head, weights, 1, 5)) / total).astype(jnp.bfloat16)

    everything = land.at[:, 0 : len(flows) + (3 if crossed else 2)]
    remote(everything, everything, recv_sems.at[0, 0], partner).wait_send()


def shards(groups, ranks, *operands):
    queries, _, _, tile_links, link_counts = operands
    rows, features = queries.shape
    tiles = tile_links.shape[0]
    slots = 4 + groups
    heads = features // HD
    bounds = [0]
    for part in CHUNK_SIXTEENTHS:
        bounds.append(bounds[-1] + part * heads // 16)
    chunks = len(bounds) - 1
    hbm = pl.BlockSpec(memory_space=pl.ANY)
    return pl.pallas_call(
        functools.partial(kernel, groups, ranks, tuple(bounds)),
        out_shape=jax.ShapeDtypeStruct((rows, features), jnp.bfloat16),
        in_specs=[hbm] * 5,
        out_specs=pl.BlockSpec(memory_space=pltpu.VMEM),
        scratch_shapes=[
            pltpu.VMEM((2, slots, rows, features), jnp.bfloat16),
            pltpu.VMEM((rows, features), jnp.bfloat16),
            pltpu.VMEM((tiles, 1, slots * rows), jnp.float32),
            pltpu.SemaphoreType.DMA,
            pltpu.SemaphoreType.DMA((chunks, 7)),
            pltpu.SemaphoreType.REGULAR((groups + 1,)),
            pltpu.SMEM(tile_links.shape, jnp.int32),
            pltpu.SMEM(link_counts.shape, jnp.int32),
            pltpu.SemaphoreType.DMA((5,)),
        ],
        compiler_params=pltpu.CompilerParams(
            collective_id=0, has_side_effects=True, vmem_limit_bytes=28 * 2**20
        ),
    )(*(pltpu.with_memory_space_constraint(a, pltpu.HBM) for a in operands))


def solution(mesh):
    nodes = P(("group", "rank"), None)
    return jax.shard_map(
        functools.partial(shards, mesh.shape["group"], mesh.shape["rank"]),
        mesh=mesh,
        in_specs=(nodes, nodes, nodes, nodes, P(("group", "rank"))),
        out_specs=nodes,
        check_vma=False,
    )
```

time: 98.3 us -> 97.1 us (0.988)
  no operation moved by 1% of the time
where the time goes in v2:
time: 97.1 us; the launch traced here: 96.9 us
  Pallas kernels  95.9 us (99%)
    pallas_call x1, Pallas kernels, shards(): pl.pallas_call(functools.partial(kernel, groups, ranks, tuple(bounds)), o...  95.9 us

profile of v2, /device:TPU:1, one launch (start us, length us, event | category | flops | bytes accessed | tf_op | source)
XLA Modules:
  0.0 96.9 jit_solution(4588175948767498754)
XLA Ops:
  0.0 95.9 %shard_map.55 = bf16[256,2048]{1,0:T(8,128)(2,1)S(1)} custom-call(bf16[256,2048]{1,0:T(8,128)(2,1)} %q_hbm.1, bf16[256,2048]{1,0:T(8,128)(2,1)} %k_hbm.1, bf16[256,2048]{1,0:T(8,128)(2,1)} %v_hbm.1, s32[2,8]{1,0:T(2,128)} %links_hbm.1, s32[2]{0:T(128)} %counts_hbm.1), custom_call_target="tpu_custom_call" | custom-call | tf_op jit(solution)/shard_map/pallas_call | solution.py:313
  95.9 1.0 %copy.7 = bf16[256,2048]{1,0:T(8,128)(2,1)} copy(bf16[256,2048]{1,0:T(8,128)(2,1)S(1)} %shard_map.55) | data formatting | bytes 2097152

commit v3 on v2

--- a/solution.py
+++ b/solution.py
@@ -11,7 +11,8 @@
 HD = 128
 CHUNK_SIXTEENTHS = (9, 5, 1, 1)
 MESH = pl.DeviceIdType.MESH
-NEAR, ACROSS_K, ACROSS_V, REST, NEAR_V, REST_V, LATE = range(7)
+NEAR, ACROSS_K, ACROSS_V, REST = range(4)
+NEAR_V, REST_V, LATE, BEAT = range(4, 8)
 
 
 def kernel(
@@ -97,8 +98,11 @@
             device_id_type=MESH,
         )
 
+    def mark(c, kind):
+        return recv_sems.at[kind + 4 * c]
+
     def take(c, kind, ref):
-        remote(ref, ref, recv_sems.at[c, kind], partner).wait_recv()
+        remote(ref, ref, mark(c, kind), partner).wait_recv()
 
     def rest_of(c, kv):
         return REST_V if c == last and kv == 1 else REST
@@ -118,21 +122,21 @@
                 kind = rest_of(c, kv)
             src = source[kv].at[:, columns(c)]
             dst = land.at[kv, slot, :, columns(c)]
-            remote(src, dst, recv_sems.at[c, kind], device).start()
+            remote(src, dst, mark(c, kind), device).start()
 
     def flow_beside(c):
         for kv in range(2):
-            kind = NEAR_V if c == beat and c < last else rest_of(c, kv)
+            kind = BEAT if c == beat and c < last else rest_of(c, kv)
             src = source[kv].at[:, columns(c)]
             dst = land.at[kv, 2 + core, :, columns(c)]
-            remote(src, dst, recv_sems.at[c, kind], partner).start()
+            remote(src, dst, mark(last if kind == BEAT else c, kind), partner).start()
 
     def pass_beside(c, kv=slice(None)):
         own = land.at[kv, near, :, columns(c)]
         take(c, NEAR if kv == slice(None) else near_of(c, kv), own)
         kind = REST if kv != 1 else LATE
         dst = land.at[kv, 3 - core, :, columns(c)]
-        remote(own, dst, recv_sems.at[c, kind], partner).start()
+        remote(own, dst, mark(c, kind), partner).start()
 
     def pass_across(c):
         for kv in range(2 if crossed else 0):
@@ -140,7 +144,7 @@
             own = land.at[kv, peer_slot(origin, g), :, columns(c)]
             take(c, (ACROSS_K, ACROSS_V)[kv], own)
             dst = land.at[kv, peer_slot(origin, target), :, columns(c)]
-            remote(own, dst, recv_sems.at[c, rest_of(c, kv)], (target, r)).start()
+            remote(own, dst, mark(c, rest_of(c, kv)), (target, r)).start()
 
     others = slots - 3 if crossed else slots - 2
 
@@ -188,7 +192,7 @@
             flow(0, f)
 
     if beat < last:
-        take(beat, NEAR_V, land.at[:, 3 - core, :, columns(beat)])
+        take(last, BEAT, land.at[:, 3 - core, :, columns(beat)])
 
     @pl.when(second[0])
     def _():
@@ -261,10 +265,11 @@
 
     def attend_all(first, end):
         pairs = (end - first) // 2
-
-        @pl.loop(0, pairs)
-        def _(i):
-            attend([first + 2 * i, first + 2 * i + 1])
+        if pairs > 0:
+
+            @pl.loop(0, pairs)
+            def _(i):
+                attend([first + 2 * i, first + 2 * i + 1])
 
         if first + 2 * pairs < end:
             attend([end - 1])
@@ -279,7 +284,7 @@
 
     heads = [pl.ds(h * HD, HD) for h in range(bounds[last], bounds[chunks])]
     part = columns(last)
-    middle = (bounds[last - 1] + bounds[last] + 1) // 2
+    middle = (bounds[last - 1] + bounds[last]) // 2
     attend_all(bounds[last - 1], middle)
     pass_beside(last, 0)
     attend_all(middle, bounds[last])
@@ -296,7 +301,7 @@
         o_ref[:, head] = ((early + mix(head, weights, 1, 5)) / total).astype(jnp.bfloat16)
 
     everything = land.at[:, 0 : len(flows) + (3 if crossed else 2)]
-    remote(everything, everything, recv_sems.at[0, 0], partner).wait_send()
+    remote(everything, everything, recv_sems.at[0], partner).wait_send()
 
 
 def shards(groups, ranks, *operands):
@@ -320,7 +325,7 @@
             pltpu.VMEM((rows, features), jnp.bfloat16),
             pltpu.VMEM((tiles, 1, slots * rows), jnp.float32),
             pltpu.SemaphoreType.DMA,
-            pltpu.SemaphoreType.DMA((chunks, 7)),
+            pltpu.SemaphoreType.DMA((4 * chunks + 4,)),
             pltpu.SemaphoreType.REGULAR((groups + 1,)),
             pltpu.SMEM(tile_links.shape, jnp.int32),
             pltpu.SMEM(link_counts.shape, jnp.int32),

time: 97.1 us -> 97 us (level)
  no operation moved by 1% of the time
where the time goes in v3:
time: 97 us; the launch traced here: 96.8 us
  Pallas kernels  95.8 us (99%)
  local copies, waits for them, and re-layouts  0.97 us (1%)
    pallas_call x1, Pallas kernels, shards(): pl.pallas_call(functools.partial(kernel, groups, ranks, tuple(bounds)), o...  95.8 us

profile of v3, /device:TPU:1, one launch (start us, length us, event | category | flops | bytes accessed | tf_op | source)
XLA Modules:
  0.0 96.8 jit_solution(1711859990135008286)
XLA Ops:
  0.0 95.8 %shard_map.55 = bf16[256,2048]{1,0:T(8,128)(2,1)S(1)} custom-call(bf16[256,2048]{1,0:T(8,128)(2,1)} %q_hbm.1, bf16[256,2048]{1,0:T(8,128)(2,1)} %k_hbm.1, bf16[256,2048]{1,0:T(8,128)(2,1)} %v_hbm.1, s32[2,8]{1,0:T(2,128)} %links_hbm.1, s32[2]{0:T(128)} %counts_hbm.1), custom_call_target="tpu_custom_call" | custom-call | tf_op jit(solution)/shard_map/pallas_call | solution.py:318
  95.8 1.0 %copy.7 = bf16[256,2048]{1,0:T(8,128)(2,1)} copy(bf16[256,2048]{1,0:T(8,128)(2,1)S(1)} %shard_map.55) | data formatting | bytes 2097152

commit v4 on v3

--- a/solution.py
+++ b/solution.py
@@ -153,7 +153,7 @@
         take(c, REST, land.at[:, 0:expected, :, columns(c)])
 
     local = [
-        pltpu.make_async_copy(src, dst, local_sems.at[i])
+        pltpu.make_async_copy(src, dst, local_sems.at[min(i, 3)])
         for i, (src, dst) in enumerate(
             (
                 (q_hbm, q_v),
@@ -229,8 +229,10 @@
             flow_beside(c)
     for copy in local[3:]:
         copy.start()
-    for copy in local:
+    for copy in local[:3]:
         copy.wait()
+    own = land.at[:, 0]
+    pltpu.make_async_copy(own, own, local_sems.at[3]).wait()
 
     cand = lax.broadcasted_iota(jnp.int32, (1, slots * rows), 1) // tile_rows
     for i in range(tiles):
@@ -315,7 +317,7 @@
         bounds.append(bounds[-1] + part * heads // 16)
     chunks = len(bounds) - 1
     hbm = pl.BlockSpec(memory_space=pl.ANY)
-    return pl.pallas_call(
+    attended = pl.pallas_call(
         functools.partial(kernel, groups, ranks, tuple(bounds)),
         out_shape=jax.ShapeDtypeStruct((rows, features), jnp.bfloat16),
         in_specs=[hbm] * 5,
@@ -326,15 +328,37 @@
             pltpu.VMEM((tiles, 1, slots * rows), jnp.float32),
             pltpu.SemaphoreType.DMA,
             pltpu.SemaphoreType.DMA((4 * chunks + 4,)),
-            pltpu.SemaphoreType.REGULAR((groups + 1,)),
+            pltpu.SemaphoreType.REGULAR((4 if groups == 4 else groups + 1,)),
             pltpu.SMEM(tile_links.shape, jnp.int32),
             pltpu.SMEM(link_counts.shape, jnp.int32),
-            pltpu.SemaphoreType.DMA((5,)),
+            pltpu.SemaphoreType.DMA((4,)),
         ],
         compiler_params=pltpu.CompilerParams(
             collective_id=0, has_side_effects=True, vmem_limit_bytes=28 * 2**20
         ),
     )(*(pltpu.with_memory_space_constraint(a, pltpu.HBM) for a in operands))
+
+    def write(src, dst, sems):
+        parts = src.shape[0] // sems.shape[0]
+        copies = [
+            pltpu.make_async_copy(
+                src.at[pl.ds(i * parts, parts)], dst.at[pl.ds(i * parts, parts)], sems.at[i]
+            )
+            for i in range(sems.shape[0])
+        ]
+        for copy in copies:
+            copy.start()
+        for copy in copies:
+            copy.wait()
+
+    return pl.pallas_call(
+        write,
+        out_shape=jax.ShapeDtypeStruct(attended.shape, attended.dtype),
+        in_specs=[pl.BlockSpec(memory_space=pltpu.VMEM)],
+        out_specs=hbm,
+        scratch_shapes=[pltpu.SemaphoreType.DMA((1,))],
+        compiler_params=pltpu.CompilerParams(vmem_limit_bytes=2**20),
+    )(attended)
 
 
 def solution(mesh):

time: 97 us -> 96.9 us (level)
  Pallas kernels: 95.8 us -> 96.8 us
  local copies, waits for them, and re-layouts: 0.97 us -> 0 us
    pallas_call x0 -> x1, Pallas kernels: none -> 0.98 us  [shards(): pl.pallas_call(write, out_shape=jax.ShapeDtypeStruct(attended.shape, atte...]
    unnamed x1 -> x0, local copies, waits for them, and re-layouts: 0.97 us -> none
where the time goes in v4:
time: 96.9 us; the launch traced here: 96.8 us
  Pallas kernels  96.8 us (100%)
    pallas_call x1, Pallas kernels, shards(): pl.pallas_call(functools.partial(kernel, groups, ranks, tuple(bounds)), o...  95.8 us

profile of v4, /device:TPU:1, one launch (start us, length us, event | category | flops | bytes accessed | tf_op | source)
XLA Modules:
  0.0 96.8 jit_solution(12598528632558477983)
XLA Ops:
  0.0 95.8 %shard_map.55.src = bf16[256,2048]{1,0:T(8,128)(2,1)S(1)} custom-call(bf16[256,2048]{1,0:T(8,128)(2,1)} %q_hbm.1, bf16[256,2048]{1,0:T(8,128)(2,1)} %k_hbm.1, bf16[256,2048]{1,0:T(8,128)(2,1)} %v_hbm.1, s32[2,8]{1,0:T(2,128)} %links_hbm.1, s32[2]{0:T(128)} %counts_hbm.1), custom_call_target="tpu_custom_call" | custom-call | tf_op jit(solution)/shard_map/pallas_call | solution.py:320
  95.8 1.0 %shard_map.56 = bf16[256,2048]{1,0:T(8,128)(2,1)} custom-call(bf16[256,2048]{1,0:T(8,128)(2,1)S(1)} %shard_map.55.src), custom_call_target="tpu_custom_call" | custom-call | tf_op jit(solution)/shard_map/pallas_call | solution.py:354
